TPU v7x, 32 devices: a 4x4x1 block of a 4x4x8 slice. The times are simulated.
32 devices in a mesh: dp: 1 (over z), ctx: 32 (over y, x, core).
Axes of the slice: x: 4, y: 4, z: 1, core: 2. Of those that a mesh axis runs over, the one named last changes fastest.
The devices are a block of a 4x4x8 slice.
Arguments:
- queries: bfloat16 [1, 4096, 8, 128], P('dp', 'ctx')
- keys: bfloat16 [1, 4096, 1, 128], P('dp', 'ctx')
- values: bfloat16 [1, 4096, 1, 128], P('dp', 'ctx')
- grad_out: bfloat16 [1, 4096, 8, 128], P('dp', 'ctx')
Outputs:
- output 1: bfloat16 [1, 4096, 8, 128], P('dp', 'ctx')
- output 2: bfloat16 [1, 4096, 8, 128], P('dp', 'ctx')
- output 3: bfloat16 [1, 4096, 1, 128], P('dp', 'ctx')
- output 4: bfloat16 [1, 4096, 1, 128], P('dp', 'ctx')
All inputs are finite; a program needn't handle non-finite values.
Results may differ from a plain program's by a relative error of at most 0.0061449.
Values are sent between devices in bfloat16 or wider.
A program may use at most 768 MiB of HBM per device.

v0:
```python
import functools
import math

import jax
import jax.numpy as jnp
from jax import lax
from jax.experimental import pallas as pl
from jax.experimental.pallas import tpu as pltpu
from jax.sharding import PartitionSpec as P

NEG_BIG = -1e30
CHUNK = 256
LANES = 128
LAG = 2
KEY, VALUE = 0, 1
F32 = jnp.float32
BF16 = jnp.bfloat16


def dot_nt(a, b):
    return lax.dot_general(a, b, (((1,), (1,)), ((), ())), preferred_element_type=F32)


def dot_nn(a, b):
    return jnp.dot(a, b, preferred_element_type=F32)


class Tree:
    def __init__(self, side):
        self.side = side
        offsets = [(dx, dy) for dx in range(side) for dy in range(side)]
        self.order = sorted(offsets, key=lambda o: (sum(min(v, side - v) for v in o), o))
        self.slot = {o: i for i, o in enumerate(self.order)}
        self.hops = [(1, 0), (side - 1, 0), (0, 1), (0, side - 1)]

    def parent(self, tensor, off):
        side = self.side
        a, b = off if tensor == KEY else off[::-1]
        if b:
            near = b if 2 * b != side else (side - 1 if a < side // 2 else 1)
            hop = (0, 1 if 2 * near < side else side - 1)
        elif a:
            near = a if 2 * a != side else (side - 1 if tensor == KEY else 1)
            hop = (1 if 2 * near < side else side - 1, 0)
        else:
            return None
        return hop if tensor == KEY else hop[::-1]

    def children(self, tensor, off):
        side = self.side
        found = []
        for hop in self.hops:
            there = tuple((o - h) % side for o, h in zip(off, hop))
            back = tuple((-h) % side for h in hop)
            if self.parent(tensor, there) == back:
                found.append((hop, self.slot[there]))
        return found


def attn_kernel(tree, n_grp, scale, q_hbm, do_hbm, k_hbm, v_hbm, o_hbm, dq_hbm, dk_hbm, dv_hbm,
                q_s, do_s, kv_s, q_t, do_t, s_buf, m_buf, l_buf, acc_buf, d_buf, out_s, kv_out,
                part, side_in, tree_in,
                load_sem, store_sem, ag_send, ag_recv, agd_send, agd_recv, rs_send, rs_recv, rsd_send, rsd_recv):
    rows, d_head = q_s.shape
    c_len = k_hbm.shape[0]
    width = 2 * c_len
    side = tree.side
    n_slot = side * side
    dev = lax.axis_index("ctx")
    core = lax.rem(dev, 2)
    mine = dev // 2
    at_x = lax.rem(mine, side)
    at_y = mine // side
    sibling = {"ctx": mine * 2 + 1 - core}
    chunks = range(rows // CHUNK)
    to_log2 = scale * math.log2(math.e)
    own_rows = pl.ds(pl.multiple_of(core * c_len, c_len), c_len)

    def chip_at(off):
        return lax.rem(at_y + off[1], side) * side + lax.rem(at_x + off[0], side)

    def near(hop):
        return {"ctx": chip_at(hop) * 2 + core}

    loads = [
        pltpu.make_async_copy(k_hbm, kv_s.at[KEY, 0, own_rows, :], load_sem.at[0]),
        pltpu.make_async_copy(v_hbm, kv_s.at[VALUE, 0, own_rows, :], load_sem.at[1]),
        pltpu.make_async_copy(q_hbm, q_s, load_sem.at[2]),
        pltpu.make_async_copy(do_hbm, do_s, load_sem.at[3]),
    ]
    for copy in loads:
        copy.start()

    barrier = pltpu.get_barrier_semaphore()
    peers = [near(hop) for hop in tree.hops] + [sibling]
    for peer in peers:
        pl.semaphore_signal(barrier, inc=1, device_id=peer, device_id_type=pl.DeviceIdType.MESH)
    pl.semaphore_wait(barrier, len(peers))

    def remote(src, dst, send, recv, peer):
        return pltpu.make_async_remote_copy(src_ref=src, dst_ref=dst, send_sem=send, recv_sem=recv,
                                            device_id=peer, device_id_type=pl.DeviceIdType.MESH)

    def gather_copy(tensor, hop, slot, slot_there):
        return remote(kv_s.at[tensor, slot, own_rows, :], kv_s.at[tensor, slot_there, own_rows, :],
                      ag_send.at[tensor, slot_there], ag_recv.at[tensor, slot_there], near(hop))

    def gather_side(tensor, slot):
        block = kv_s.at[tensor, slot, own_rows, :]
        return remote(block, block, agd_send.at[tensor, slot], agd_recv.at[tensor, slot], sibling)

    def gather_forward(tensor, slot):
        if slot:
            gather_copy(tensor, tree.parent(tensor, tree.order[slot]), slot, slot).wait_recv()
        for hop, slot_there in tree.children(tensor, tree.order[slot]):
            gather_copy(tensor, hop, slot, slot_there).start()
        gather_side(tensor, slot).start()

    def score_step(slot):
        masked = slot == 0
        k_blk = kv_s[KEY, slot]
        for c in chunks:
            rng = pl.ds(c * CHUNK, CHUNK)
            s = dot_nt(q_s[rng, :], k_blk)
            if masked:
                tok = lax.broadcasted_iota(jnp.int32, s.shape, 0) // n_grp + (c * CHUNK // n_grp) + core * c_len
                key = lax.broadcasted_iota(jnp.int32, s.shape, 1)
                s = jnp.where(tok >= key, s, NEG_BIG)
            s_buf[slot, rng, :] = s
            m = jnp.full((CHUNK, LANES), NEG_BIG, F32) if masked else m_buf[rng, :]
            for j in range(width // LANES):
                m = jnp.maximum(m, s[:, j * LANES:(j + 1) * LANES])
            m_buf[rng, :] = m

    loads[0].wait()
    loads[1].wait()
    gather_forward(KEY, 0)
    gather_forward(VALUE, 0)
    loads[2].wait()
    loads[3].wait()
    q_t[...] = q_s[...].astype(F32).T.astype(BF16)
    do_t[...] = do_s[...].astype(F32).T.astype(BF16)
    l_buf[...] = jnp.zeros(l_buf.shape, F32)
    acc_buf[...] = jnp.zeros(acc_buf.shape, F32)

    for step in range(n_slot + 1):
        if 0 < step < n_slot:
            gather_forward(KEY, step)
            gather_forward(VALUE, step)
        if step:
            slot = step - 1
            gather_side(KEY, slot).wait_recv()
            pl.when(chip_at(tree.order[slot]) <= mine)(functools.partial(score_step, slot))
    for slot in range(n_slot):
        gather_side(VALUE, slot).wait_recv()

    for c in chunks:
        rng = pl.ds(c * CHUNK, CHUNK)
        m = jnp.max(m_buf[rng, :], axis=1, keepdims=True) * to_log2
        m_buf[rng, :] = jnp.broadcast_to(m, (CHUNK, LANES))

    xs = sum(o[0] << (2 * i) for i, o in enumerate(tree.order))
    ys = sum(o[1] << (2 * i) for i, o in enumerate(tree.order))

    def slot_chip(slot):
        def field(packed):
            signed = packed - (1 << 32) if packed >= 1 << 31 else packed
            return lax.shift_right_logical(jnp.int32(signed), 2 * slot) & 3
        return chip_at((field(xs), field(ys)))

    def value_step(slot):
        v_blk = kv_s[VALUE, slot]
        for c in chunks:
            rng = pl.ds(c * CHUNK, CHUNK)
            m = m_buf[rng, :]
            w = jnp.exp2(s_buf[slot, rng, :] * to_log2 - jnp.concatenate([m] * (width // LANES), axis=1))
            s_buf[slot, rng, :] = w
            l = l_buf[rng, :]
            for j in range(width // LANES):
                l = l + w[:, j * LANES:(j + 1) * LANES]
            l_buf[rng, :] = l
            acc_buf[rng, :] += dot_nn(w.astype(BF16), v_blk)

    @pl.loop(0, n_slot)
    def _(slot):
        pl.when(slot_chip(slot) <= mine)(lambda: value_step(slot))

    for c in chunks:
        rng = pl.ds(c * CHUNK, CHUNK)
        l = jnp.sum(l_buf[rng, :], axis=1, keepdims=True)
        out = (acc_buf[rng, :] / l).astype(BF16)
        out_s[0, rng, :] = out
        l_buf[rng, :] = jnp.broadcast_to(1.0 / l, (CHUNK, LANES))
        delta = jnp.sum(do_s[rng, :].astype(F32) * out.astype(F32), axis=1, keepdims=True)
        d_buf[rng, :] = jnp.broadcast_to(delta, (CHUNK, LANES))
    store_o = pltpu.make_async_copy(out_s.at[0], o_hbm, store_sem.at[0])
    store_o.start()
    acc_buf[...] = jnp.zeros(acc_buf.shape, F32)

    def side_copy(tensor, slot):
        return remote(part.at[tensor, slot, 1 - core], side_in.at[tensor, slot],
                      rsd_send.at[tensor, slot], rsd_recv.at[tensor, slot], sibling)

    def tree_copy(tensor, slot):
        hop = tree.parent(tensor, tree.order[slot])
        return remote(part.at[tensor, slot, core], tree_in.at[tensor, slot],
                      rs_send.at[tensor, slot], rs_recv.at[tensor, slot], near(hop))

    def grad_step(slot):
        k_blk = kv_s[KEY, slot]
        v_blk = kv_s[VALUE, slot]
        dv = jnp.zeros((d_head, width), F32)
        dk = jnp.zeros((d_head, width), F32)
        for c in chunks:
            rng = pl.ds(c * CHUNK, CHUNK)
            inv = jnp.concatenate([l_buf[rng, :]] * (width // LANES), axis=1)
            delta = jnp.concatenate([d_buf[rng, :]] * (width // LANES), axis=1)
            p = s_buf[slot, rng, :] * inv
            dp = dot_nt(do_s[rng, :], v_blk)
            ds = (p * (dp - delta)).astype(BF16)
            dv = dv + dot_nn(do_t[:, rng], p.astype(BF16))
            dk = dk + dot_nn(q_t[:, rng], ds)
            acc_buf[rng, :] += dot_nn(ds, k_blk)
        for h in range(2):
            part[KEY, slot, h] = dk[:, h * c_len:(h + 1) * c_len]
            part[VALUE, slot, h] = dv[:, h * c_len:(h + 1) * c_len]

    def zero_step(slot):
        part[:, slot] = jnp.zeros(part.shape[:1] + part.shape[2:], F32)

    def merge(slot):
        for tensor in (KEY, VALUE):
            side_copy(tensor, slot).wait_recv()
            total = part[tensor, slot, core] + side_in[tensor, slot]
            for _, child in tree.children(tensor, tree.order[slot]):
                tree_copy(tensor, child).wait_recv()
                total = total + tree_in[tensor, child]
            if slot:
                part[tensor, slot, core] = total
                tree_copy(tensor, slot).start()
            else:
                total = total * scale if tensor == KEY else total
                kv_out[tensor] = total.T.astype(BF16)

    @pl.loop(0, n_slot)
    def _(step):
        slot = n_slot - 1 - step
        active = slot_chip(slot) <= mine
        pl.when(active)(lambda: grad_step(slot))
        pl.when(jnp.logical_not(active))(lambda: zero_step(slot))
        for tensor in (KEY, VALUE):
            side_copy_dyn = remote(part.at[tensor, slot, 1 - core], side_in.at[tensor, slot],
                                   rsd_send.at[tensor, slot], rsd_recv.at[tensor, slot], sibling)
            side_copy_dyn.start()
        for s in range(LAG, n_slot):
            pl.when(slot == s - LAG)(functools.partial(merge, s))

    for c in chunks:
        rng = pl.ds(c * CHUNK, CHUNK)
        out_s[1, rng, :] = (acc_buf[rng, :] * scale).astype(BF16)
    store_dq = pltpu.make_async_copy(out_s.at[1], dq_hbm, store_sem.at[1])
    store_dq.start()
    for s in reversed(range(LAG)):
        merge(s)
    store_dk = pltpu.make_async_copy(kv_out.at[KEY], dk_hbm, store_sem.at[2])
    store_dv = pltpu.make_async_copy(kv_out.at[VALUE], dv_hbm, store_sem.at[3])
    store_dk.start()
    store_dv.start()

    for tensor in (KEY, VALUE):
        for slot in range(n_slot):
            gather_side(tensor, slot).wait_send()
            side_copy(tensor, slot).wait_send()
            for hop, slot_there in tree.children(tensor, tree.order[slot]):
                gather_copy(tensor, hop, slot, slot_there).wait_send()
            if slot:
                tree_copy(tensor, slot).wait_send()
    for copy in (store_o, store_dq, store_dk, store_dv):
        copy.wait()


def solution(mesh):
    part_spec = P("dp", "ctx")
    n_dev = mesh.shape["ctx"]
    tree = Tree(math.isqrt(n_dev // 2))

    def local_step(queries, keys, values, grad_out):
        n_batch, c_len, n_q, d_head = queries.shape
        n_kv = keys.shape[2]
        n_grp = n_q // n_kv
        rows = c_len * n_q
        width = 2 * c_len
        n_slot = n_dev // 2
        scale = d_head ** -0.5
        blocks = (2, n_slot)
        any_spec = pl.BlockSpec(memory_space=pl.ANY)
        out, dq, dk, dv = pl.pallas_call(
            functools.partial(attn_kernel, tree, n_grp, scale),
            out_shape=(
                jax.ShapeDtypeStruct((rows, d_head), BF16),
                jax.ShapeDtypeStruct((rows, d_head), BF16),
                jax.ShapeDtypeStruct((c_len, d_head), BF16),
                jax.ShapeDtypeStruct((c_len, d_head), BF16),
            ),
            in_specs=[any_spec] * 4,
            out_specs=[any_spec] * 4,
            scratch_shapes=[
                pltpu.VMEM((rows, d_head), BF16),
                pltpu.VMEM((rows, d_head), BF16),
                pltpu.VMEM(blocks + (width, d_head), BF16),
                pltpu.VMEM((d_head, rows), BF16),
                pltpu.VMEM((d_head, rows), BF16),
                pltpu.VMEM((n_slot, rows, width), F32),
                pltpu.VMEM((rows, LANES), F32),
                pltpu.VMEM((rows, LANES), F32),
                pltpu.VMEM((rows, d_head), F32),
                pltpu.VMEM((rows, LANES), F32),
                pltpu.VMEM((2, rows, d_head), BF16),
                pltpu.VMEM((2, c_len, d_head), BF16),
                pltpu.VMEM(blocks + (2, d_head, c_len), F32),
                pltpu.VMEM(blocks + (d_head, c_len), F32),
                pltpu.VMEM(blocks + (d_head, c_len), F32),
                pltpu.SemaphoreType.DMA((4,)),
                pltpu.SemaphoreType.DMA((4,)),
            ] + [pltpu.SemaphoreType.DMA(blocks)] * 8,
            compiler_params=pltpu.CompilerParams(
                vmem_limit_bytes=60 * 1024 * 1024, collective_id=0, has_side_effects=True),
            name="attn",
        )(queries.reshape(rows, d_head), grad_out.reshape(rows, d_head),
          keys.reshape(c_len, d_head), values.reshape(c_len, d_head))
        q_shape = (n_batch, c_len, n_q, d_head)
        kv_shape = (n_batch, c_len, n_kv, d_head)
        return out.reshape(q_shape), dq.reshape(q_shape), dk.reshape(kv_shape), dv.reshape(kv_shape)

    return jax.shard_map(local_step, mesh=mesh, in_specs=(part_spec,) * 4, out_specs=(part_spec,) * 4, check_vma=False)
```

profile of v0, /device:TPU:97, one launch (start us, length us, event | category | flops | bytes accessed | tf_op | source)
XLA Modules:
  0.0 60.0 jit_solution(6333500262011770460)
XLA Ops:
  0.6 55.5 %attn.1 = (bf16[1024,128]{1,0:T(8,128)(2,1)}, bf16[1024,128]{1,0:T(8,128)(2,1)}, bf16[128,128]{1,0:T(8,128)(2,1)}, bf16[128,128]{1,0:T(8,128)(2,1)}) custom-call(bf16[1024,128]{1,0:T(8,128)(2,1)} %bitcast.8, bf16[1024,128]{1,0:T(8,128)(2,1)} %bitcast.9, bf16[128,128]{1,0:T(8,128)(2,1)} %bitcast.12, bf16[128,128]{1,0:T(8,128)(2,1)} %bitcast.13), custom_call_target="tpu_custom_call" | custom-call | tf_op jit(solution)/shard_map/attn/pallas_call | solution.py:297
  56.2 0.0 copy-start
  56.2 1.7 %copy.12 = bf16[1,128,8,128]{3,2,1,0:T(8,128)(2,1)} copy(bf16[1,128,8,128]{3,2,1,0:T(8,128)(2,1)} %bitcast.11) | data formatting | bytes 524288
  57.9 0.0 copy-done
  57.9 0.0 copy-start.2
  57.9 0.7 %copy.13 = bf16[1,128,8,128]{3,2,1,0:T(8,128)(2,1)} copy(bf16[1,128,8,128]{3,2,1,0:T(8,128)(2,1)S(1)} %bitcast.10) | data formatting | bytes 524288
  58.6 0.1 copy-done.2
  58.6 0.0 copy-start.1
  58.6 0.6 %copy.14 = bf16[1,128,1,128]{3,1,2,0:T(8,128)(2,1)} copy(bf16[1,128,1,128]{3,1,2,0:T(8,128)(2,1)S(1)} %bitcast.15) | data formatting | bytes 65536
  59.3 0.2 copy-done.1
  59.4 0.6 %copy.15 = bf16[1,128,1,128]{3,1,2,0:T(8,128)(2,1)} copy(bf16[1,128,1,128]{3,1,2,0:T(8,128)(2,1)S(1)} %bitcast.14) | data formatting | bytes 65536
Async XLA Ops:
  56.2 1.7 %copy-start = (bf16[1024,128]{1,0:T(8,128)(2,1)S(1)}, bf16[1024,128]{1,0:T(8,128)(2,1)}, u32[]{:S(2)}) copy-start(bf16[1024,128]{1,0:T(8,128)(2,1)} %get-tuple-element.9) | copy-start | bytes 786436
  57.9 0.8 %copy-start.2 = (bf16[128,128]{1,0:T(8,128)(2,1)S(1)}, bf16[128,128]{1,0:T(8,128)(2,1)}, u32[]{:S(2)}) copy-start(bf16[128,128]{1,0:T(8,128)(2,1)} %get-tuple-element.10) | copy-start | bytes 98308
  58.6 0.8 %copy-start.1 = (bf16[128,128]{1,0:T(8,128)(2,1)S(1)}, bf16[128,128]{1,0:T(8,128)(2,1)}, u32[]{:S(2)}) copy-start(bf16[128,128]{1,0:T(8,128)(2,1)} %get-tuple-element.11) | copy-start | bytes 98308
where the time goes:
time: 60.3 us; the launch traced here: 60 us
  Pallas kernels  55.5 us (92%)
  local copies, waits for them, and re-layouts  3.86 us (6%)
  between operations  0.65 us (1%)
    pallas_call x1, Pallas kernels, local_step(): pl.pallas_call(functools.partial(attn_kernel, tree, n_grp, scale), out_sh...  55.5 us
    unnamed x10, local copies, waits for them, and re-layouts  3.86 us

commit v1 on v0

v1 whole, which is shorter than its diff:
```python
import functools
import math

import jax
import jax.numpy as jnp
from jax import lax
from jax.experimental import pallas as pl
from jax.experimental.pallas import tpu as pltpu
from jax.sharding import PartitionSpec as P

NEG_BIG = -1e30
CHUNK = 256
LANES = 128
LAG = 2
QUERIES = {11: 1, 9: 1, 4: 2}
KEY, VALUE = 0, 1
F32 = jnp.float32
BF16 = jnp.bfloat16


def dot_nt(a, b):
    return lax.dot_general(a, b, (((1,), (1,)), ((), ())), preferred_element_type=F32)


def dot_nn(a, b):
    return jnp.dot(a, b, preferred_element_type=F32)


class Tree:
    def __init__(self, side):
        self.side = side
        offsets = [(dx, dy) for dx in range(side) for dy in range(side)]
        length = lambda v: min(v, side - v)
        self.order = sorted(offsets, key=lambda o: (length(o[0]) + length(o[1]), length(o[0]) == 2 or length(o[1]) == 2, o))
        self.slot = {o: i for i, o in enumerate(self.order)}
        self.n_near = sum(length(o[0]) < 2 and length(o[1]) < 2 for o in offsets)
        self.hops = [(1, 0), (side - 1, 0), (0, 1), (0, side - 1)]

    def parent(self, tensor, off):
        side = self.side
        a, b = off if tensor == KEY else off[::-1]
        if b:
            near = b if 2 * b != side else (side - 1 if a < side // 2 else 1)
            hop = (0, 1 if 2 * near < side else side - 1)
        elif a:
            near = a if 2 * a != side else (side - 1 if tensor == KEY else 1)
            hop = (1 if 2 * near < side else side - 1, 0)
        else:
            return None
        return hop if tensor == KEY else hop[::-1]

    def children(self, tensor, off):
        found = []
        for hop in self.hops:
            there = tuple((o - h) % self.side for o, h in zip(off, hop))
            back = tuple((-h) % self.side for h in hop)
            if there != (0, 0) and self.parent(tensor, there) == back:
                found.append(self.slot[there])
        return found

    def source(self, off):
        side = self.side
        mid, one, far = side // 2, 1, side - 1
        if mid not in off:
            return off
        if off == (mid, mid):
            return (one, one)
        if off[0] == mid:
            return (one if off[1] == 0 else far, 0)
        return (0, one if off[0] == 0 else far)

    def targets(self, slot):
        found = []
        for there in range(1, len(self.order)):
            src = self.source(self.order[there])
            if tuple((o - e) % self.side for o, e in zip(self.order[there], src)) == self.order[slot]:
                found.append((tuple((-e) % self.side for e in src), there))
        return found


    def takers(self, slot):
        found = [(0, 0)]
        for off, there in self.targets(slot):
            found += [self.move(off, o) for o in self.takers(there)]
        return found

    def givers(self, tensor, slot):
        found = [(0, 0)]
        for child in self.children(tensor, self.order[slot]):
            hop = self.hop_to(slot, child)
            found += [self.move(hop, o) for o in self.givers(tensor, child)]
        return found

    def move(self, a, b):
        return tuple((i + j) % self.side for i, j in zip(a, b))

    def hop_to(self, slot, child):
        return tuple((i - j) % self.side for i, j in zip(self.order[slot], self.order[child]))


def attn_kernel(tree, n_grp, scale, q_hbm, do_hbm, k_hbm, v_hbm, o_hbm, dq_hbm, dk_hbm, dv_hbm,
                q_s, do_s, kv_s, q_t, do_t, s_buf, dp_buf, ds_buf, m_buf, top_buf, l_buf, acc_buf, d_buf, out_s, kv_out,
                part, side_in, tree_in, local_sem, gather_sem, cross_sem, side_sem, tree_sem, sent_sem):
    rows, d_head = q_s.shape
    c_len = k_hbm.shape[0]
    width = 2 * c_len
    side = tree.side
    n_slot = side * side
    n_near = tree.n_near
    dev = lax.axis_index("ctx")
    core = lax.rem(dev, 2)
    mine = dev // 2
    at_x = lax.rem(mine, side)
    at_y = mine // side
    sibling = {"ctx": mine * 2 + 1 - core}
    chunks = [pl.ds(i * CHUNK, CHUNK) for i in range(rows // CHUNK)]
    to_log2 = scale * math.log2(math.e)
    own_rows = pl.ds(pl.multiple_of(core * c_len, c_len), c_len)

    def chip_at(off):
        return lax.rem(at_y + off[1], side) * side + lax.rem(at_x + off[0], side)

    def near(off):
        return {"ctx": chip_at(off) * 2 + core}

    def wide(x):
        return jnp.concatenate([x] * (width // LANES), axis=1)

    loads = [
        pltpu.make_async_copy(k_hbm, kv_s.at[0, KEY, own_rows, :], local_sem.at[0]),
        pltpu.make_async_copy(v_hbm, kv_s.at[0, VALUE, own_rows, :], local_sem.at[1]),
        pltpu.make_async_copy(q_hbm, q_s, local_sem.at[2]),
        pltpu.make_async_copy(do_hbm, do_s, local_sem.at[3]),
    ]
    for copy in loads:
        copy.start()

    with jax.named_scope("barrier"):
        barrier = pltpu.get_barrier_semaphore()
        peers = [near(off) for off in tree.order[1:n_near]] + [sibling]
        for peer in peers:
            pl.semaphore_signal(barrier, inc=1, device_id=peer, device_id_type=pl.DeviceIdType.MESH)
        pl.semaphore_wait(barrier, len(peers))

    def remote(src, dst, send, recv, peer):
        return pltpu.make_async_remote_copy(src_ref=src, dst_ref=dst, send_sem=send, recv_sem=recv,
                                            device_id=peer, device_id_type=pl.DeviceIdType.MESH)

    def gather_copy(slot, off, there):
        return remote(kv_s.at[slot, :, own_rows, :], kv_s.at[there, :, own_rows, :],
                      sent_sem.at[0, there], gather_sem.at[there], near(off))

    def cross_copy(slot):
        block = kv_s.at[slot, :, own_rows, :]
        return remote(block, block, sent_sem.at[1, slot], cross_sem.at[slot], sibling)

    def side_copy(slot):
        return remote(part.at[slot, 1 - core], side_in.at[slot], sent_sem.at[1, slot], side_sem.at[slot], sibling)

    def tree_copy(tensor, slot):
        hop = tree.parent(tensor, tree.order[slot])
        return remote(part.at[slot, core, tensor], tree_in.at[tensor, slot],
                      sent_sem.at[2 * tensor, slot], tree_sem.at[tensor, slot], near(hop))

    def concerns(slot, offsets):
        owner = chip_at(tree.order[slot])
        return functools.reduce(jnp.logical_or, [chip_at(o) >= owner for o in offsets])

    def taken(slot, off, there):
        return concerns(slot, [tree.move(off, o) for o in tree.takers(there)])

    def given(tensor, slot, child):
        return concerns(slot, [tree.move(tree.hop_to(slot, child), o) for o in tree.givers(tensor, child)])

    def active(slot):
        return slot_chip(slot) <= mine

    def each_target(slot, act):
        for off, there in tree.targets(slot):
            pl.when(taken(slot, off, there))(functools.partial(act, slot, off, there))

    def arrive(first, last):
        for slot in range(first, last):
            if slot:
                pl.when(concerns(slot, tree.takers(slot)))(
                    gather_copy(slot, tree.source(tree.order[slot]), slot).wait_recv)
            each_target(slot, lambda *which: gather_copy(*which).start())
            pl.when(active(slot))(cross_copy(slot).start)

    xs = sum(o[0] << (2 * i) for i, o in enumerate(tree.order))
    ys = sum(o[1] << (2 * i) for i, o in enumerate(tree.order))

    def slot_chip(slot):
        def field(packed):
            signed = packed - (1 << 32) if packed >= 1 << 31 else packed
            return lax.shift_right_logical(jnp.int32(signed), 2 * slot) & 3
        return chip_at((field(xs), field(ys)))

    def score_step(slot, masked):
        k_blk = kv_s[slot, KEY]
        v_blk = kv_s[slot, VALUE]
        for c, rng in enumerate(chunks):
            s = dot_nt(q_s[rng, :], k_blk)
            if masked:
                tok = lax.broadcasted_iota(jnp.int32, s.shape, 0) // n_grp + (c * CHUNK // n_grp) + core * c_len
                key = lax.broadcasted_iota(jnp.int32, s.shape, 1)
                s = jnp.where(tok >= key, s, NEG_BIG)
            s_buf[slot, rng, :] = s
            m = jnp.full((CHUNK, LANES), NEG_BIG, F32) if masked else m_buf[rng, :]
            for j in range(width // LANES):
                m = jnp.maximum(m, s[:, j * LANES:(j + 1) * LANES])
            m_buf[rng, :] = m
            dp_buf[slot, rng, :] = dot_nt(do_s[rng, :], v_blk)

    def value_step(slot):
        v_blk = kv_s[slot, VALUE]
        for rng in chunks:
            w = jnp.exp2(s_buf[slot, rng, :] * to_log2 - wide(top_buf[rng, :]))
            l = l_buf[rng, :]
            for j in range(width // LANES):
                l = l + w[:, j * LANES:(j + 1) * LANES]
            l_buf[rng, :] = l
            acc_buf[rng, :] += dot_nn(w.astype(BF16), v_blk)

    def top_step(again):
        for rng in chunks:
            top = jnp.max(m_buf[rng, :], axis=1, keepdims=True) * to_log2
            top = jnp.broadcast_to(top, (CHUNK, LANES))
            if again:
                shrink = jnp.exp2(top_buf[rng, :] - top)
                l_buf[rng, :] = l_buf[rng, :] * shrink
                acc_buf[rng, :] = acc_buf[rng, :] * shrink
            top_buf[rng, :] = top

    def score_loop(first, last):
        @pl.loop(first, last)
        def _(slot):
            @pl.when(active(slot))
            def _():
                cross_copy(slot).wait_recv()
                score_step(slot, False)

    def value_loop(first, last):
        @pl.loop(first, last)
        def _(slot):
            @pl.when(active(slot))
            def _():
                value_step(slot)
                cross_copy(slot).wait_send()

    loads[0].wait()
    loads[1].wait()
    arrive(0, 1)
    loads[2].wait()
    loads[3].wait()
    with jax.named_scope("first"):
        q_t[...] = q_s[...].astype(F32).T.astype(BF16)
        do_t[...] = do_s[...].astype(F32).T.astype(BF16)
        l_buf[...] = jnp.zeros(l_buf.shape, F32)
        acc_buf[...] = jnp.zeros(acc_buf.shape, F32)
        cross_copy(0).wait_recv()
        score_step(0, True)

    n_next = len(tree.hops) + 1
    with jax.named_scope("arrive_next"):
        arrive(1, n_next)
    with jax.named_scope("score_next"):
        score_loop(1, n_next)
    with jax.named_scope("arrive_near"):
        arrive(n_next, n_near)
    with jax.named_scope("score_near"):
        score_loop(n_next, n_near)
    with jax.named_scope("value_near"):
        top_step(False)
        value_loop(0, n_near)
    with jax.named_scope("arrive_far"):
        arrive(n_near, n_slot)
    with jax.named_scope("score_far"):
        score_loop(n_near, n_slot)
    with jax.named_scope("value_far"):
        top_step(True)
        value_loop(n_near, n_slot)

    with jax.named_scope("out"):
        for rng in chunks:
            l = jnp.sum(l_buf[rng, :], axis=1, keepdims=True)
            out = (acc_buf[rng, :] / l).astype(BF16)
            out_s[0, rng, :] = out
            top_buf[rng, :] = top_buf[rng, :] + jnp.broadcast_to(jnp.log2(l), (CHUNK, LANES))
            delta = jnp.sum(do_s[rng, :].astype(F32) * out.astype(F32), axis=1, keepdims=True)
            d_buf[rng, :] = jnp.broadcast_to(delta, (CHUNK, LANES))
        store_o = pltpu.make_async_copy(out_s.at[0], o_hbm, local_sem.at[0])
        store_o.start()
        acc_buf[...] = jnp.zeros(acc_buf.shape, F32)
        for slot in range(n_near):
            each_target(slot, lambda *which: gather_copy(*which).wait_send())

    def grad_step(slot):
        dv = jnp.zeros((d_head, width), F32)
        dk = jnp.zeros((d_head, width), F32)
        for rng in chunks:
            p = jnp.exp2(s_buf[slot, rng, :] * to_log2 - wide(top_buf[rng, :]))
            ds = (p * (dp_buf[slot, rng, :] - wide(d_buf[rng, :]))).astype(BF16)
            ds_buf[slot, rng, :] = ds
            dv = dv + dot_nn(do_t[:, rng], p.astype(BF16))
            dk = dk + dot_nn(q_t[:, rng], ds)
        for h in range(2):
            part[slot, h, KEY] = dk[:, h * c_len:(h + 1) * c_len]
            part[slot, h, VALUE] = dv[:, h * c_len:(h + 1) * c_len]

    def zero_step(slot):
        part[slot] = jnp.zeros(part.shape[1:], F32)

    def merge(slot):
        @pl.when(active(slot))
        def _():
            side_copy(slot).wait_recv()
            part[slot, core] = part[slot, core] + side_in[slot]

        for tensor in (KEY, VALUE):
            for child in tree.children(tensor, tree.order[slot]):
                @pl.when(given(tensor, slot, child))
                def _():
                    tree_copy(tensor, child).wait_recv()
                    part[slot, core, tensor] = part[slot, core, tensor] + tree_in[tensor, child]
            if slot:
                pl.when(concerns(slot, tree.givers(tensor, slot)))(tree_copy(tensor, slot).start)
        if slot == 0:
            kv_out[KEY] = (part[0, core, KEY] * scale).T.astype(BF16)
            kv_out[VALUE] = part[0, core, VALUE].T.astype(BF16)

    def sums_sent(first, last):
        for slot in range(first, last):
            for tensor in (KEY, VALUE):
                pl.when(concerns(slot, tree.givers(tensor, slot)))(tree_copy(tensor, slot).wait_send)

    def query_step(slot):
        k_blk = kv_s[slot, KEY]
        for rng in chunks:
            acc_buf[rng, :] += dot_nn(ds_buf[slot, rng, :], k_blk)

    def query_loop(first, last):
        if first < last:
            with jax.named_scope(f"query#n={last - first}"):
                @pl.loop(first, last)
                def _(slot):
                    pl.when(active(slot))(lambda: query_step(slot))

    left = n_slot
    before = {}
    for slot in reversed(range(n_slot)):
        taken = min(QUERIES.get(slot, 0), left)
        before[slot] = (left - taken, left)
        left -= taken

    def merge_after_queries(slot):
        query_loop(*before[slot])
        with jax.named_scope(f"merge#s={slot}"):
            merge(slot)

    @pl.loop(0, n_slot)
    def _(step):
        slot = n_slot - 1 - step

        @pl.when(active(slot))
        def _():
            with jax.named_scope("grad"):
                grad_step(slot)
            side_copy(slot).start()

        pl.when(jnp.logical_not(active(slot)))(lambda: zero_step(slot))
        for s in range(LAG, n_slot):
            pl.when(slot == s - LAG)(functools.partial(merge_after_queries, s))

    for s in reversed(range(1, LAG)):
        merge_after_queries(s)
    query_loop(0, left)
    with jax.named_scope("query_out"):
        for rng in chunks:
            out_s[1, rng, :] = (acc_buf[rng, :] * scale).astype(BF16)
        store_dq = pltpu.make_async_copy(out_s.at[1], dq_hbm, local_sem.at[1])
        store_dq.start()
    with jax.named_scope("drain"):
        sums_sent(len(tree.hops) + 1, n_slot)

        @pl.loop(0, n_slot)
        def _(slot):
            pl.when(active(slot))(lambda: side_copy(slot).wait_send())

    with jax.named_scope("merge#s=0"):
        merge(0)
    store_dk = pltpu.make_async_copy(kv_out.at[KEY], dk_hbm, local_sem.at[2])
    store_dv = pltpu.make_async_copy(kv_out.at[VALUE], dv_hbm, local_sem.at[3])
    store_dk.start()
    store_dv.start()
    sums_sent(1, len(tree.hops) + 1)
    with jax.named_scope("store"):
        for copy in (store_o, store_dq, store_dk, store_dv):
            copy.wait()


def solution(mesh):
    part_spec = P("dp", "ctx")
    n_dev = mesh.shape["ctx"]
    tree = Tree(math.isqrt(n_dev // 2))

    def local_step(queries, keys, values, grad_out):
        n_batch, c_len, n_q, d_head = queries.shape
        n_kv = keys.shape[2]
        n_grp = n_q // n_kv
        rows = c_len * n_q
        width = 2 * c_len
        n_slot = n_dev // 2
        scale = d_head ** -0.5
        any_spec = pl.BlockSpec(memory_space=pl.ANY)
        dma_sem = pltpu.SemaphoreType.DMA
        out, dq, dk, dv = pl.pallas_call(
            functools.partial(attn_kernel, tree, n_grp, scale),
            out_shape=(
                jax.ShapeDtypeStruct((rows, d_head), BF16),
                jax.ShapeDtypeStruct((rows, d_head), BF16),
                jax.ShapeDtypeStruct((c_len, d_head), BF16),
                jax.ShapeDtypeStruct((c_len, d_head), BF16),
            ),
            in_specs=[any_spec] * 4,
            out_specs=[any_spec] * 4,
            scratch_shapes=[
                pltpu.VMEM((rows, d_head), BF16),
                pltpu.VMEM((rows, d_head), BF16),
                pltpu.VMEM((n_slot, 2, width, d_head), BF16),
                pltpu.VMEM((d_head, rows), BF16),
                pltpu.VMEM((d_head, rows), BF16),
                pltpu.VMEM((n_slot, rows, width), F32),
                pltpu.VMEM((n_slot, rows, width), F32),
                pltpu.VMEM((n_slot, rows, width), BF16),
                pltpu.VMEM((rows, LANES), F32),
                pltpu.VMEM((rows, LANES), F32),
                pltpu.VMEM((rows, LANES), F32),
                pltpu.VMEM((rows, d_head), F32),
                pltpu.VMEM((rows, LANES), F32),
                pltpu.VMEM((2, rows, d_head), BF16),
                pltpu.VMEM((2, c_len, d_head), BF16),
                pltpu.VMEM((n_slot, 2, 2, d_head, c_len), F32),
                pltpu.VMEM((n_slot, 2, d_head, c_len), F32),
                pltpu.VMEM((2, n_slot, d_head, c_len), F32),
                dma_sem((4,)),
                dma_sem((n_slot,)),
                dma_sem((n_slot,)),
                dma_sem((n_slot,)),
                dma_sem((2, n_slot)),
                dma_sem((3, n_slot)),
            ],
            compiler_params=pltpu.CompilerParams(
                vmem_limit_bytes=60 * 1024 * 1024, collective_id=0, has_side_effects=True),
            name="attn",
        )(queries.reshape(rows, d_head), grad_out.reshape(rows, d_head),
          keys.reshape(c_len, d_head), values.reshape(c_len, d_head))
        q_shape = (n_batch, c_len, n_q, d_head)
        kv_shape = (n_batch, c_len, n_kv, d_head)
        return out.reshape(q_shape), dq.reshape(q_shape), dk.reshape(kv_shape), dv.reshape(kv_shape)

    return jax.shard_map(local_step, mesh=mesh, in_specs=(part_spec,) * 4, out_specs=(part_spec,) * 4, check_vma=False)
```

time: 60.3 us -> 54.9 us (0.910)
  Pallas kernels: 55.5 us -> 50.1 us
    pallas_call x1, Pallas kernels: 55.5 us -> 50.1 us  [local_step(): pl.pallas_call(functools.partial(attn_kernel, tree, n_grp, scale), out_sh...]
where the time goes in v1:
time: 54.9 us; the launch traced here: 54.6 us
  Pallas kernels  50.1 us (91%)
  local copies, waits for them, and re-layouts  3.86 us (7%)
  between operations  0.65 us (1%)
    pallas_call x1, Pallas kernels, local_step(): pl.pallas_call(functools.partial(attn_kernel, tree, n_grp, scale), out_sh...  50.1 us
    unnamed x10, local copies, waits for them, and re-layouts  3.86 us

profile of v1, /device:TPU:97, one launch (start us, length us, event | category | flops | bytes accessed | tf_op | source)
XLA Modules:
  0.0 54.6 jit_solution(14320901627713887814)
XLA Ops:
  0.6 50.1 %attn.1 = (bf16[1024,128]{1,0:T(8,128)(2,1)}, bf16[1024,128]{1,0:T(8,128)(2,1)}, bf16[128,128]{1,0:T(8,128)(2,1)}, bf16[128,128]{1,0:T(8,128)(2,1)}) custom-call(bf16[1024,128]{1,0:T(8,128)(2,1)} %bitcast.8, bf16[1024,128]{1,0:T(8,128)(2,1)} %bitcast.9, bf16[128,128]{1,0:T(8,128)(2,1)} %bitcast.12, bf16[128,128]{1,0:T(8,128)(2,1)} %bitcast.13), custom_call_target="tpu_custom_call" | custom-call | tf_op jit(solution)/shard_map/attn/pallas_call | solution.py:417
  50.8 0.0 copy-start
  50.8 1.7 %copy.12 = bf16[1,128,8,128]{3,2,1,0:T(8,128)(2,1)} copy(bf16[1,128,8,128]{3,2,1,0:T(8,128)(2,1)} %bitcast.11) | data formatting | bytes 524288
  52.5 0.0 copy-done
  52.5 0.0 copy-start.2
  52.5 0.7 %copy.13 = bf16[1,128,8,128]{3,2,1,0:T(8,128)(2,1)} copy(bf16[1,128,8,128]{3,2,1,0:T(8,128)(2,1)S(1)} %bitcast.10) | data formatting | bytes 524288
  53.2 0.1 copy-done.2
  53.3 0.0 copy-start.1
  53.3 0.6 %copy.14 = bf16[1,128,1,128]{3,1,2,0:T(8,128)(2,1)} copy(bf16[1,128,1,128]{3,1,2,0:T(8,128)(2,1)S(1)} %bitcast.15) | data formatting | bytes 65536
  53.9 0.2 copy-done.1
  54.0 0.6 %copy.15 = bf16[1,128,1,128]{3,1,2,0:T(8,128)(2,1)} copy(bf16[1,128,1,128]{3,1,2,0:T(8,128)(2,1)S(1)} %bitcast.14) | data formatting | bytes 65536
Async XLA Ops:
  50.8 1.7 %copy-start = (bf16[1024,128]{1,0:T(8,128)(2,1)S(1)}, bf16[1024,128]{1,0:T(8,128)(2,1)}, u32[]{:S(2)}) copy-start(bf16[1024,128]{1,0:T(8,128)(2,1)} %get-tuple-element.9) | copy-start | bytes 786436
  52.5 0.8 %copy-start.2 = (bf16[128,128]{1,0:T(8,128)(2,1)S(1)}, bf16[128,128]{1,0:T(8,128)(2,1)}, u32[]{:S(2)}) copy-start(bf16[128,128]{1,0:T(8,128)(2,1)} %get-tuple-element.10) | copy-start | bytes 98308
  53.3 0.8 %copy-start.1 = (bf16[128,128]{1,0:T(8,128)(2,1)S(1)}, bf16[128,128]{1,0:T(8,128)(2,1)}, u32[]{:S(2)}) copy-start(bf16[128,128]{1,0:T(8,128)(2,1)} %get-tuple-element.11) | copy-start | bytes 98308

commit v2 on v1

--- a/solution.py
+++ b/solution.py
@@ -10,20 +10,28 @@
 
 NEG_BIG = -1e30
 CHUNK = 256
-LANES = 128
+SUBLANES = 8
 LAG = 2
-QUERIES = {11: 1, 9: 1, 4: 2}
+QUERIES = {}
 KEY, VALUE = 0, 1
 F32 = jnp.float32
 BF16 = jnp.bfloat16
 
 
-def dot_nt(a, b):
-    return lax.dot_general(a, b, (((1,), (1,)), ((), ())), preferred_element_type=F32)
+def dot_tn(a, b):
+    return lax.dot_general(a, b, (((0,), (0,)), ((), ())), preferred_element_type=F32)
 
 
 def dot_nn(a, b):
     return jnp.dot(a, b, preferred_element_type=F32)
+
+
+def fold(x):
+    return x.reshape(x.shape[0] // SUBLANES, SUBLANES, x.shape[1])
+
+
+def spread(x):
+    return jnp.broadcast_to(x, (SUBLANES, x.shape[1]))
 
 
 class Tree:
@@ -38,25 +46,23 @@
 
     def parent(self, tensor, off):
         side = self.side
-        a, b = off if tensor == KEY else off[::-1]
-        if b:
-            near = b if 2 * b != side else (side - 1 if a < side // 2 else 1)
-            hop = (0, 1 if 2 * near < side else side - 1)
-        elif a:
-            near = a if 2 * a != side else (side - 1 if tensor == KEY else 1)
-            hop = (1 if 2 * near < side else side - 1, 0)
-        else:
+        mid, one, far = side // 2, 1, side - 1
+        first, last = (one, far) if tensor == KEY else (far, one)
+        if off == (0, 0):
             return None
-        return hop if tensor == KEY else hop[::-1]
+        if off == (mid, mid):
+            return (first, first)
+        if off[0] == mid:
+            return (first if off[1] in (0, one) else last, 0)
+        if off[1] == mid:
+            return (0, last if off[0] in (0, far) else first)
+        if 0 in off:
+            return off
+        return (0, off[1]) if tensor == KEY else (off[0], 0)
 
     def children(self, tensor, off):
-        found = []
-        for hop in self.hops:
-            there = tuple((o - h) % self.side for o, h in zip(off, hop))
-            back = tuple((-h) % self.side for h in hop)
-            if there != (0, 0) and self.parent(tensor, there) == back:
-                found.append(self.slot[there])
-        return found
+        return [there for there in range(1, len(self.order)) if off == tuple(
+            (o - p) % self.side for o, p in zip(self.order[there], self.parent(tensor, self.order[there])))]
 
     def source(self, off):
         side = self.side
@@ -98,8 +104,8 @@
         return tuple((i - j) % self.side for i, j in zip(self.order[slot], self.order[child]))
 
 
-def attn_kernel(tree, n_grp, scale, q_hbm, do_hbm, k_hbm, v_hbm, o_hbm, dq_hbm, dk_hbm, dv_hbm,
-                q_s, do_s, kv_s, q_t, do_t, s_buf, dp_buf, ds_buf, m_buf, top_buf, l_buf, acc_buf, d_buf, out_s, kv_out,
+def attn_kernel(tree, n_grp, scale, q_hbm, do_hbm, k_hbm, v_hbm, o_out, dq_out, dk_out, dv_out,
+                q_s, do_s, kv_s, q_t, do_t, s_buf, dp_buf, ds_buf, m_buf, top_buf, l_buf, acc_buf, d_buf,
                 part, side_in, tree_in, local_sem, gather_sem, cross_sem, side_sem, tree_sem, sent_sem):
     rows, d_head = q_s.shape
     c_len = k_hbm.shape[0]
@@ -123,9 +129,6 @@
     def near(off):
         return {"ctx": chip_at(off) * 2 + core}
 
-    def wide(x):
-        return jnp.concatenate([x] * (width // LANES), axis=1)
-
     loads = [
         pltpu.make_async_copy(k_hbm, kv_s.at[0, KEY, own_rows, :], local_sem.at[0]),
         pltpu.make_async_copy(v_hbm, kv_s.at[0, VALUE, own_rows, :], local_sem.at[1]),
@@ -200,37 +203,31 @@
         k_blk = kv_s[slot, KEY]
         v_blk = kv_s[slot, VALUE]
         for c, rng in enumerate(chunks):
-            s = dot_nt(q_s[rng, :], k_blk)
+            s = dot_nn(k_blk, q_t[:, rng])
             if masked:
-                tok = lax.broadcasted_iota(jnp.int32, s.shape, 0) // n_grp + (c * CHUNK // n_grp) + core * c_len
-                key = lax.broadcasted_iota(jnp.int32, s.shape, 1)
+                key = lax.broadcasted_iota(jnp.int32, s.shape, 0)
+                tok = lax.broadcasted_iota(jnp.int32, s.shape, 1) // n_grp + (c * CHUNK // n_grp) + core * c_len
                 s = jnp.where(tok >= key, s, NEG_BIG)
-            s_buf[slot, rng, :] = s
-            m = jnp.full((CHUNK, LANES), NEG_BIG, F32) if masked else m_buf[rng, :]
-            for j in range(width // LANES):
-                m = jnp.maximum(m, s[:, j * LANES:(j + 1) * LANES])
-            m_buf[rng, :] = m
-            dp_buf[slot, rng, :] = dot_nt(do_s[rng, :], v_blk)
+            s_buf[slot, :, rng] = s
+            m = jnp.max(fold(s), axis=0)
+            m_buf[:, rng] = m if masked else jnp.maximum(m_buf[:, rng], m)
+            dp_buf[slot, :, rng] = dot_nn(v_blk, do_t[:, rng])
 
     def value_step(slot):
         v_blk = kv_s[slot, VALUE]
         for rng in chunks:
-            w = jnp.exp2(s_buf[slot, rng, :] * to_log2 - wide(top_buf[rng, :]))
-            l = l_buf[rng, :]
-            for j in range(width // LANES):
-                l = l + w[:, j * LANES:(j + 1) * LANES]
-            l_buf[rng, :] = l
-            acc_buf[rng, :] += dot_nn(w.astype(BF16), v_blk)
+            w = jnp.exp2(fold(s_buf[slot, :, rng]) * to_log2 - top_buf[:, rng])
+            l_buf[:, rng] += jnp.sum(w, axis=0)
+            acc_buf[:, rng] += dot_tn(v_blk, w.reshape(width, CHUNK).astype(BF16))
 
     def top_step(again):
         for rng in chunks:
-            top = jnp.max(m_buf[rng, :], axis=1, keepdims=True) * to_log2
-            top = jnp.broadcast_to(top, (CHUNK, LANES))
+            top = spread(jnp.max(m_buf[:, rng], axis=0, keepdims=True) * to_log2)
             if again:
-                shrink = jnp.exp2(top_buf[rng, :] - top)
-                l_buf[rng, :] = l_buf[rng, :] * shrink
-                acc_buf[rng, :] = acc_buf[rng, :] * shrink
-            top_buf[rng, :] = top
+                shrink = jnp.exp2(top_buf[:, rng] - top)
+                l_buf[:, rng] = l_buf[:, rng] * shrink
+                acc_buf[:, rng] = (fold(acc_buf[:, rng]) * shrink).reshape(d_head, CHUNK)
+            top_buf[:, rng] = top
 
     def score_loop(first, last):
         @pl.loop(first, last)
@@ -283,30 +280,28 @@
 
     with jax.named_scope("out"):
         for rng in chunks:
-            l = jnp.sum(l_buf[rng, :], axis=1, keepdims=True)
-            out = (acc_buf[rng, :] / l).astype(BF16)
-            out_s[0, rng, :] = out
-            top_buf[rng, :] = top_buf[rng, :] + jnp.broadcast_to(jnp.log2(l), (CHUNK, LANES))
-            delta = jnp.sum(do_s[rng, :].astype(F32) * out.astype(F32), axis=1, keepdims=True)
-            d_buf[rng, :] = jnp.broadcast_to(delta, (CHUNK, LANES))
-        store_o = pltpu.make_async_copy(out_s.at[0], o_hbm, local_sem.at[0])
-        store_o.start()
+            l = spread(jnp.sum(l_buf[:, rng], axis=0, keepdims=True))
+            out = (fold(acc_buf[:, rng]) / l).reshape(d_head, CHUNK).astype(BF16).astype(F32)
+            o_out[rng, :] = out.T.astype(BF16)
+            top_buf[:, rng] = top_buf[:, rng] + jnp.log2(l)
+            d_buf[:, rng] = spread(jnp.sum(do_t[:, rng].astype(F32) * out, axis=0, keepdims=True))
         acc_buf[...] = jnp.zeros(acc_buf.shape, F32)
         for slot in range(n_near):
             each_target(slot, lambda *which: gather_copy(*which).wait_send())
 
     def grad_step(slot):
-        dv = jnp.zeros((d_head, width), F32)
-        dk = jnp.zeros((d_head, width), F32)
-        for rng in chunks:
-            p = jnp.exp2(s_buf[slot, rng, :] * to_log2 - wide(top_buf[rng, :]))
-            ds = (p * (dp_buf[slot, rng, :] - wide(d_buf[rng, :]))).astype(BF16)
-            ds_buf[slot, rng, :] = ds
-            dv = dv + dot_nn(do_t[:, rng], p.astype(BF16))
-            dk = dk + dot_nn(q_t[:, rng], ds)
+        dv = jnp.zeros((width, d_head), F32)
+        dk = jnp.zeros((width, d_head), F32)
+        for rng in chunks:
+            p = jnp.exp2(fold(s_buf[slot, :, rng]) * to_log2 - top_buf[:, rng])
+            ds = p * (fold(dp_buf[slot, :, rng]) - d_buf[:, rng])
+            ds = ds.reshape(width, CHUNK).astype(BF16)
+            ds_buf[slot, :, rng] = ds
+            dv = dv + dot_nn(p.reshape(width, CHUNK).astype(BF16), do_s[rng, :])
+            dk = dk + dot_nn(ds, q_s[rng, :])
         for h in range(2):
-            part[slot, h, KEY] = dk[:, h * c_len:(h + 1) * c_len]
-            part[slot, h, VALUE] = dv[:, h * c_len:(h + 1) * c_len]
+            part[slot, h, KEY] = dk[h * c_len:(h + 1) * c_len, :]
+            part[slot, h, VALUE] = dv[h * c_len:(h + 1) * c_len, :]
 
     def zero_step(slot):
         part[slot] = jnp.zeros(part.shape[1:], F32)
@@ -326,8 +321,8 @@
             if slot:
                 pl.when(concerns(slot, tree.givers(tensor, slot)))(tree_copy(tensor, slot).start)
         if slot == 0:
-            kv_out[KEY] = (part[0, core, KEY] * scale).T.astype(BF16)
-            kv_out[VALUE] = part[0, core, VALUE].T.astype(BF16)
+            dk_out[...] = (part[0, core, KEY] * scale).astype(BF16)
+            dv_out[...] = part[0, core, VALUE].astype(BF16)
 
     def sums_sent(first, last):
         for slot in range(first, last):
@@ -337,7 +332,7 @@
     def query_step(slot):
         k_blk = kv_s[slot, KEY]
         for rng in chunks:
-            acc_buf[rng, :] += dot_nn(ds_buf[slot, rng, :], k_blk)
+            acc_buf[:, rng] += dot_tn(k_blk, ds_buf[slot, :, rng])
 
     def query_loop(first, last):
         if first < last:
@@ -377,9 +372,7 @@
     query_loop(0, left)
     with jax.named_scope("query_out"):
         for rng in chunks:
-            out_s[1, rng, :] = (acc_buf[rng, :] * scale).astype(BF16)
-        store_dq = pltpu.make_async_copy(out_s.at[1], dq_hbm, local_sem.at[1])
-        store_dq.start()
+            dq_out[rng, :] = (acc_buf[:, rng] * scale).T.astype(BF16)
     with jax.named_scope("drain"):
         sums_sent(len(tree.hops) + 1, n_slot)
 
@@ -389,14 +382,17 @@
 
     with jax.named_scope("merge#s=0"):
         merge(0)
-    store_dk = pltpu.make_async_copy(kv_out.at[KEY], dk_hbm, local_sem.at[2])
-    store_dv = pltpu.make_async_copy(kv_out.at[VALUE], dv_hbm, local_sem.at[3])
-    store_dk.start()
-    store_dv.start()
     sums_sent(1, len(tree.hops) + 1)
-    with jax.named_scope("store"):
-        for copy in (store_o, store_dq, store_dk, store_dv):
-            copy.wait()
+
+
+def store_kernel(*refs):
+    *pairs, sem = refs
+    half = len(pairs) // 2
+    copies = [pltpu.make_async_copy(src, dst, sem.at[i]) for i, (src, dst) in enumerate(zip(pairs[:half], pairs[half:]))]
+    for copy in copies:
+        copy.start()
+    for copy in copies:
+        copy.wait()
 
 
 def solution(mesh):
@@ -414,35 +410,29 @@
         scale = d_head ** -0.5
         any_spec = pl.BlockSpec(memory_space=pl.ANY)
         dma_sem = pltpu.SemaphoreType.DMA
-        out, dq, dk, dv = pl.pallas_call(
+        shapes = [(rows, d_head)] * 2 + [(c_len, d_head)] * 2
+        results = pl.pallas_call(
             functools.partial(attn_kernel, tree, n_grp, scale),
-            out_shape=(
-                jax.ShapeDtypeStruct((rows, d_head), BF16),
-                jax.ShapeDtypeStruct((rows, d_head), BF16),
-                jax.ShapeDtypeStruct((c_len, d_head), BF16),
-                jax.ShapeDtypeStruct((c_len, d_head), BF16),
-            ),
+            out_shape=[pltpu.VMEM(shape, BF16) for shape in shapes],
             in_specs=[any_spec] * 4,
-            out_specs=[any_spec] * 4,
+            out_specs=[pl.BlockSpec(memory_space=pltpu.VMEM)] * 4,
             scratch_shapes=[
                 pltpu.VMEM((rows, d_head), BF16),
                 pltpu.VMEM((rows, d_head), BF16),
                 pltpu.VMEM((n_slot, 2, width, d_head), BF16),
                 pltpu.VMEM((d_head, rows), BF16),
                 pltpu.VMEM((d_head, rows), BF16),
-                pltpu.VMEM((n_slot, rows, width), F32),
-                pltpu.VMEM((n_slot, rows, width), F32),
-                pltpu.VMEM((n_slot, rows, width), BF16),
-                pltpu.VMEM((rows, LANES), F32),
-                pltpu.VMEM((rows, LANES), F32),
-                pltpu.VMEM((rows, LANES), F32),
-                pltpu.VMEM((rows, d_head), F32),
-                pltpu.VMEM((rows, LANES), F32),
-                pltpu.VMEM((2, rows, d_head), BF16),
-                pltpu.VMEM((2, c_len, d_head), BF16),
-                pltpu.VMEM((n_slot, 2, 2, d_head, c_len), F32),
-                pltpu.VMEM((n_slot, 2, d_head, c_len), F32),
-                pltpu.VMEM((2, n_slot, d_head, c_len), F32),
+                pltpu.VMEM((n_slot, width, rows), F32),
+                pltpu.VMEM((n_slot, width, rows), F32),
+                pltpu.VMEM((n_slot, width, rows), BF16),
+                pltpu.VMEM((SUBLANES, rows), F32),
+                pltpu.VMEM((SUBLANES, rows), F32),
+                pltpu.VMEM((SUBLANES, rows), F32),
+                pltpu.VMEM((d_head, rows), F32),
+                pltpu.VMEM((SUBLANES, rows), F32),
+                pltpu.VMEM((n_slot, 2, 2, c_len, d_head), F32),
+                pltpu.VMEM((n_slot, 2, c_len, d_head), F32),
+                pltpu.VMEM((2, n_slot, c_len, d_head), F32),
                 dma_sem((4,)),
                 dma_sem((n_slot,)),
                 dma_sem((n_slot,)),
@@ -455,6 +445,15 @@
             name="attn",
         )(queries.reshape(rows, d_head), grad_out.reshape(rows, d_head),
           keys.reshape(c_len, d_head), values.reshape(c_len, d_head))
+        out, dq, dk, dv = pl.pallas_call(
+            store_kernel,
+            out_shape=[jax.ShapeDtypeStruct(shape, BF16) for shape in shapes],
+            in_specs=[pl.BlockSpec(memory_space=pltpu.VMEM)] * 4,
+            out_specs=[any_spec] * 4,
+            scratch_shapes=[dma_sem((4,))],
+            compiler_params=pltpu.CompilerParams(vmem_limit_bytes=2 * 1024 * 1024),
+            name="store",
+        )(*results)
         q_shape = (n_batch, c_len, n_q, d_head)
         kv_shape = (n_batch, c_len, n_kv, d_head)
         return out.reshape(q_shape), dq.reshape(q_shape), dk.reshape(kv_shape), dv.reshape(kv_shape)

time: 54.9 us -> 47.9 us (0.87); the launches traced: 54.6 us -> 47 us
  local copies, waits for them, and re-layouts: 3.86 us -> 0 us
  Pallas kernels: 50.1 us -> 46.4 us
    pallas_call x1, Pallas kernels: 50.1 us -> 45.5 us  [local_step(): pl.pallas_call(functools.partial(attn_kernel, tree, n_grp, scale), out_sh...]
    unnamed x10 -> x0, local copies, waits for them, and re-layouts: 3.86 us -> none
    pallas_call x0 -> x1, Pallas kernels: none -> 0.84 us  [local_step(): pl.pallas_call(store_kernel, out_shape=[jax.ShapeDtypeStruct(shape, BF16)...]
where the time goes in v2:
time: 47.9 us; the launch traced here: 47 us
  Pallas kernels  46.4 us (97%)
  between operations  0.64 us (1%)
    pallas_call x1, Pallas kernels, local_step(): pl.pallas_call(functools.partial(attn_kernel, tree, n_grp, scale), out_sh...  45.5 us

profile of v2, /device:TPU:97, one launch (start us, length us, event | category | flops | bytes accessed | tf_op | source)
XLA Modules:
  0.0 47.0 jit_solution(115043978375665970)
XLA Ops:
  0.6 45.5 %attn.1 = (bf16[1024,128]{1,0:T(8,128)(2,1)S(1)}, bf16[1024,128]{1,0:T(8,128)(2,1)S(1)}, bf16[128,128]{1,0:T(8,128)(2,1)S(1)}, bf16[128,128]{1,0:T(8,128)(2,1)S(1)}) custom-call(bf16[1024,128]{1,0:T(8,128)(2,1)} %bitcast.8, bf16[1024,128]{1,0:T(8,128)(2,1)} %bitcast.9, bf16[128,128]{1,0:T(8,128)(2,1)} %bitcast.10, bf16[128,128]{1,0:T(8,128)(2,1)} %bitcast.11), custom_call_target="tpu_custom_call" | custom-call | tf_op jit(solution)/shard_map/attn/pallas_call | solution.py:414
  46.2 0.8 %store.1 = (bf16[1024,128]{1,0:T(8,128)(2,1)}, bf16[1024,128]{1,0:T(8,128)(2,1)}, bf16[128,128]{1,0:T(8,128)(2,1)}, bf16[128,128]{1,0:T(8,128)(2,1)}) custom-call(bf16[1024,128]{1,0:T(8,128)(2,1)S(1)} %get-tuple-element.12.refs_0_, bf16[1024,128]{1,0:T(8,128)(2,1)S(1)} %get-tuple-element.13.refs_1_, bf16[128,128]{1,0:T(8,128)(2,1)S(1)} %get-tuple-element.14.refs_2_, ...), custom_call_target="tpu_custom_call" | custom-call | tf_op jit(solution)/shard_map/store/pallas_call | solution.py:448

commit v3 on v2

--- a/solution.py
+++ b/solution.py
@@ -11,11 +11,20 @@
 NEG_BIG = -1e30
 CHUNK = 256
 SUBLANES = 8
-LAG = 2
-QUERIES = {}
 KEY, VALUE = 0, 1
 F32 = jnp.float32
 BF16 = jnp.bfloat16
+GRAD, SUM, QUERY = 0, 1, 2
+PLAN = (
+    (GRAD, 15), (GRAD, 11), (GRAD, 7), (GRAD, 12), (SUM, 15), (SUM, 11), (GRAD, 13), (GRAD, 10), (SUM, 12),
+    (GRAD, 9), (SUM, 13), (QUERY, 2), (SUM, 10), (GRAD, 3), (SUM, 7), (SUM, 9), (GRAD, 14), (GRAD, 1), (GRAD, 8),
+    (SUM, 14), (SUM, 1), (QUERY, 2), (GRAD, 5), (GRAD, 2), (SUM, 8), (GRAD, 0), (SUM, 5), (GRAD, 6), (GRAD, 4),
+    (QUERY, 2), (SUM, 6), (QUERY, 2), (QUERY, 2), (SUM, 2), (SUM, 4), (QUERY, 2), (QUERY, 2), (QUERY, 2), (SUM, 3),
+)
+PARENTS = (
+    (None, (0, 1), (0, 3), (1, 0), (3, 0), (1, 1), (0, 3), (0, 1), (3, 0), (0, 3), (1, 0), (0, 1), (1, 0), (3, 0), (3, 3), (1, 1)),
+    (None, (0, 1), (0, 3), (1, 0), (3, 0), (1, 1), (1, 3), (0, 1), (3, 0), (0, 3), (3, 0), (0, 3), (1, 0), (1, 0), (3, 3), (3, 3)),
+)
 
 
 def dot_tn(a, b):
@@ -38,27 +47,21 @@
     def __init__(self, side):
         self.side = side
         offsets = [(dx, dy) for dx in range(side) for dy in range(side)]
-        length = lambda v: min(v, side - v)
-        self.order = sorted(offsets, key=lambda o: (length(o[0]) + length(o[1]), length(o[0]) == 2 or length(o[1]) == 2, o))
+        mid = side // 2
+
+        def group(o):
+            if mid in o:
+                return 3 if 0 in o else 5 if o == (mid, mid) else 4
+            return 0 if o == (0, 0) else 1 if 0 in o else 2
+
+        self.order = sorted(offsets, key=lambda o: (group(o), o))
+        kinds = [group(o) for o in self.order]
+        self.bounds = [kinds.index(k) for k in range(5)] + [len(kinds)]
+        self.n_near = self.bounds[3]
         self.slot = {o: i for i, o in enumerate(self.order)}
-        self.n_near = sum(length(o[0]) < 2 and length(o[1]) < 2 for o in offsets)
-        self.hops = [(1, 0), (side - 1, 0), (0, 1), (0, side - 1)]
 
     def parent(self, tensor, off):
-        side = self.side
-        mid, one, far = side // 2, 1, side - 1
-        first, last = (one, far) if tensor == KEY else (far, one)
-        if off == (0, 0):
-            return None
-        if off == (mid, mid):
-            return (first, first)
-        if off[0] == mid:
-            return (first if off[1] in (0, one) else last, 0)
-        if off[1] == mid:
-            return (0, last if off[0] in (0, far) else first)
-        if 0 in off:
-            return off
-        return (0, off[1]) if tensor == KEY else (off[0], 0)
+        return PARENTS[tensor][self.slot[off]]
 
     def children(self, tensor, off):
         return [there for there in range(1, len(self.order)) if off == tuple(
@@ -105,7 +108,7 @@
 
 
 def attn_kernel(tree, n_grp, scale, q_hbm, do_hbm, k_hbm, v_hbm, o_out, dq_out, dk_out, dv_out,
-                q_s, do_s, kv_s, q_t, do_t, s_buf, dp_buf, ds_buf, m_buf, top_buf, l_buf, acc_buf, d_buf,
+                q_s, do_s, kv_s, q_t, do_t, s_buf, dp_buf, ds_buf, p_buf, m_buf, top_buf, l_buf, acc_buf, d_buf,
                 part, side_in, tree_in, local_sem, gather_sem, cross_sem, side_sem, tree_sem, sent_sem):
     rows, d_head = q_s.shape
     c_len = k_hbm.shape[0]
@@ -176,7 +179,8 @@
         return concerns(slot, [tree.move(tree.hop_to(slot, child), o) for o in tree.givers(tensor, child)])
 
     def active(slot):
-        return slot_chip(slot) <= mine
+        owner = chip_at(tree.order[slot]) if isinstance(slot, int) else slot_chip(slot)
+        return owner <= mine
 
     def each_target(slot, act):
         for off, there in tree.targets(slot):
@@ -199,26 +203,31 @@
             return lax.shift_right_logical(jnp.int32(signed), 2 * slot) & 3
         return chip_at((field(xs), field(ys)))
 
-    def score_step(slot, masked):
-        k_blk = kv_s[slot, KEY]
-        v_blk = kv_s[slot, VALUE]
+    def score_step(slots, masked):
         for c, rng in enumerate(chunks):
-            s = dot_nn(k_blk, q_t[:, rng])
-            if masked:
-                key = lax.broadcasted_iota(jnp.int32, s.shape, 0)
-                tok = lax.broadcasted_iota(jnp.int32, s.shape, 1) // n_grp + (c * CHUNK // n_grp) + core * c_len
-                s = jnp.where(tok >= key, s, NEG_BIG)
-            s_buf[slot, :, rng] = s
-            m = jnp.max(fold(s), axis=0)
-            m_buf[:, rng] = m if masked else jnp.maximum(m_buf[:, rng], m)
-            dp_buf[slot, :, rng] = dot_nn(v_blk, do_t[:, rng])
-
-    def value_step(slot):
-        v_blk = kv_s[slot, VALUE]
-        for rng in chunks:
-            w = jnp.exp2(fold(s_buf[slot, :, rng]) * to_log2 - top_buf[:, rng])
-            l_buf[:, rng] += jnp.sum(w, axis=0)
-            acc_buf[:, rng] += dot_tn(v_blk, w.reshape(width, CHUNK).astype(BF16))
+            m = None if masked else m_buf[:, rng]
+            for slot in slots:
+                s = dot_nn(kv_s[slot, KEY], q_t[:, rng])
+                if masked:
+                    key = lax.broadcasted_iota(jnp.int32, s.shape, 0)
+                    tok = lax.broadcasted_iota(jnp.int32, s.shape, 1) // n_grp + (c * CHUNK // n_grp) + core * c_len
+                    s = jnp.where(tok >= key, s, NEG_BIG)
+                s_buf[slot, :, rng] = s
+                top = jnp.max(fold(s), axis=0)
+                m = top if m is None else jnp.maximum(m, top)
+                dp_buf[slot, :, rng] = dot_nn(kv_s[slot, VALUE], do_t[:, rng])
+            m_buf[:, rng] = m
+
+    def value_step(slots):
+        for rng in chunks:
+            l = l_buf[:, rng]
+            acc = acc_buf[:, rng]
+            for slot in slots:
+                w = jnp.exp2(fold(s_buf[slot, :, rng]) * to_log2 - top_buf[:, rng])
+                l = l + jnp.sum(w, axis=0)
+                acc = acc + dot_tn(kv_s[slot, VALUE], w.reshape(width, CHUNK).astype(BF16))
+            l_buf[:, rng] = l
+            acc_buf[:, rng] = acc
 
     def top_step(again):
         for rng in chunks:
@@ -229,21 +238,33 @@
                 acc_buf[:, rng] = (fold(acc_buf[:, rng]) * shrink).reshape(d_head, CHUNK)
             top_buf[:, rng] = top
 
+    def pair_loop(first, last, body):
+        @pl.loop(0, (last - first) // 2)
+        def _(i):
+            a, b = first + 2 * i, first + 2 * i + 1
+            both = jnp.logical_and(active(a), active(b))
+            pl.when(both)(lambda: body([a, b]))
+            for slot in (a, b):
+                pl.when(jnp.logical_and(active(slot), jnp.logical_not(both)))(functools.partial(body, [slot]))
+
+        if (last - first) % 2:
+            pl.when(active(last - 1))(lambda: body([last - 1]))
+
+    def score_body(slots):
+        for slot in slots:
+            cross_copy(slot).wait_recv()
+        score_step(slots, False)
+
+    def value_body(slots):
+        value_step(slots)
+        for slot in slots:
+            cross_copy(slot).wait_send()
+
     def score_loop(first, last):
-        @pl.loop(first, last)
-        def _(slot):
-            @pl.when(active(slot))
-            def _():
-                cross_copy(slot).wait_recv()
-                score_step(slot, False)
+        pair_loop(first, last, score_body)
 
     def value_loop(first, last):
-        @pl.loop(first, last)
-        def _(slot):
-            @pl.when(active(slot))
-            def _():
-                value_step(slot)
-                cross_copy(slot).wait_send()
+        pair_loop(first, last, value_body)
 
     loads[0].wait()
     loads[1].wait()
@@ -256,17 +277,14 @@
         l_buf[...] = jnp.zeros(l_buf.shape, F32)
         acc_buf[...] = jnp.zeros(acc_buf.shape, F32)
         cross_copy(0).wait_recv()
-        score_step(0, True)
-
-    n_next = len(tree.hops) + 1
-    with jax.named_scope("arrive_next"):
-        arrive(1, n_next)
-    with jax.named_scope("score_next"):
-        score_loop(1, n_next)
-    with jax.named_scope("arrive_near"):
-        arrive(n_next, n_near)
-    with jax.named_scope("score_near"):
-        score_loop(n_next, n_near)
+        score_step([0], True)
+
+    n_next = tree.bounds[2]
+    for first, last in ((1, n_next), (n_next, n_near)):
+        with jax.named_scope(f"arrive#s={first}"):
+            arrive(first, last)
+        with jax.named_scope(f"score#s={first}"):
+            score_loop(first, last)
     with jax.named_scope("value_near"):
         top_step(False)
         value_loop(0, n_near)
@@ -290,18 +308,15 @@
             each_target(slot, lambda *which: gather_copy(*which).wait_send())
 
     def grad_step(slot):
-        dv = jnp.zeros((width, d_head), F32)
-        dk = jnp.zeros((width, d_head), F32)
         for rng in chunks:
             p = jnp.exp2(fold(s_buf[slot, :, rng]) * to_log2 - top_buf[:, rng])
             ds = p * (fold(dp_buf[slot, :, rng]) - d_buf[:, rng])
-            ds = ds.reshape(width, CHUNK).astype(BF16)
-            ds_buf[slot, :, rng] = ds
-            dv = dv + dot_nn(p.reshape(width, CHUNK).astype(BF16), do_s[rng, :])
-            dk = dk + dot_nn(ds, q_s[rng, :])
+            p_buf[:, rng] = p.reshape(width, CHUNK).astype(BF16)
+            ds_buf[slot, :, rng] = ds.reshape(width, CHUNK).astype(BF16)
         for h in range(2):
-            part[slot, h, KEY] = dk[h * c_len:(h + 1) * c_len, :]
-            part[slot, h, VALUE] = dv[h * c_len:(h + 1) * c_len, :]
+            keys = pl.ds(h * c_len, c_len)
+            part[slot, h, KEY] = dot_nn(ds_buf[slot, keys, :], q_s[...])
+            part[slot, h, VALUE] = dot_nn(p_buf[keys, :], do_s[...])
 
     def zero_step(slot):
         part[slot] = jnp.zeros(part.shape[1:], F32)
@@ -324,57 +339,50 @@
             dk_out[...] = (part[0, core, KEY] * scale).astype(BF16)
             dv_out[...] = part[0, core, VALUE].astype(BF16)
 
-    def sums_sent(first, last):
-        for slot in range(first, last):
+    def sums_sent(slots):
+        for slot in slots:
             for tensor in (KEY, VALUE):
                 pl.when(concerns(slot, tree.givers(tensor, slot)))(tree_copy(tensor, slot).wait_send)
 
-    def query_step(slot):
-        k_blk = kv_s[slot, KEY]
-        for rng in chunks:
-            acc_buf[:, rng] += dot_tn(k_blk, ds_buf[slot, :, rng])
-
-    def query_loop(first, last):
-        if first < last:
-            with jax.named_scope(f"query#n={last - first}"):
-                @pl.loop(first, last)
-                def _(slot):
-                    pl.when(active(slot))(lambda: query_step(slot))
-
-    left = n_slot
-    before = {}
-    for slot in reversed(range(n_slot)):
-        taken = min(QUERIES.get(slot, 0), left)
-        before[slot] = (left - taken, left)
-        left -= taken
-
-    def merge_after_queries(slot):
-        query_loop(*before[slot])
-        with jax.named_scope(f"merge#s={slot}"):
-            merge(slot)
-
-    @pl.loop(0, n_slot)
-    def _(step):
-        slot = n_slot - 1 - step
-
-        @pl.when(active(slot))
-        def _():
-            with jax.named_scope("grad"):
-                grad_step(slot)
-            side_copy(slot).start()
-
-        pl.when(jnp.logical_not(active(slot)))(lambda: zero_step(slot))
-        for s in range(LAG, n_slot):
-            pl.when(slot == s - LAG)(functools.partial(merge_after_queries, s))
-
-    for s in reversed(range(1, LAG)):
-        merge_after_queries(s)
-    query_loop(0, left)
-    with jax.named_scope("query_out"):
+    def query_step(slots):
+        for rng in chunks:
+            acc = acc_buf[:, rng]
+            for slot in slots:
+                acc = acc + dot_tn(kv_s[slot, KEY], ds_buf[slot, :, rng])
+            acc_buf[:, rng] = acc
+
+    def queries(slots):
+        for a, b in zip(slots[::2], slots[1::2]):
+            both = jnp.logical_and(active(a), active(b))
+            pl.when(both)(functools.partial(query_step, [a, b]))
+            for slot in (a, b):
+                pl.when(jnp.logical_and(active(slot), jnp.logical_not(both)))(functools.partial(query_step, [slot]))
+        if len(slots) % 2:
+            pl.when(active(slots[-1]))(functools.partial(query_step, [slots[-1]]))
+
+    order = [which for what, which in PLAN if what == GRAD]
+    sums = [which for what, which in PLAN if what == SUM]
+    asked = 0
+    for what, which in PLAN:
+        if what == GRAD:
+            with jax.named_scope(f"grad#s={which}"):
+                pl.when(active(which))(functools.partial(grad_step, which))
+                pl.when(jnp.logical_not(active(which)))(functools.partial(zero_step, which))
+            pl.when(active(which))(side_copy(which).start)
+        elif what == SUM:
+            with jax.named_scope(f"merge#s={which}"):
+                merge(which)
+        else:
+            with jax.named_scope(f"query#n={which}"):
+                queries(order[asked:asked + which])
+            asked += which
+
+    with jax.named_scope("query"):
+        queries(order[asked:])
         for rng in chunks:
             dq_out[rng, :] = (acc_buf[:, rng] * scale).T.astype(BF16)
     with jax.named_scope("drain"):
-        sums_sent(len(tree.hops) + 1, n_slot)
+        sums_sent(sums[:-4])
 
         @pl.loop(0, n_slot)
         def _(slot):
@@ -382,7 +390,7 @@
 
     with jax.named_scope("merge#s=0"):
         merge(0)
-    sums_sent(1, len(tree.hops) + 1)
+    sums_sent(sums[-4:])
 
 
 def store_kernel(*refs):
@@ -425,6 +433,7 @@
                 pltpu.VMEM((n_slot, width, rows), F32),
                 pltpu.VMEM((n_slot, width, rows), F32),
                 pltpu.VMEM((n_slot, width, rows), BF16),
+                pltpu.VMEM((width, rows), BF16),
                 pltpu.VMEM((SUBLANES, rows), F32),
                 pltpu.VMEM((SUBLANES, rows), F32),
                 pltpu.VMEM((SUBLANES, rows), F32),

time: 47.9 us -> 46.7 us (0.975)
  the two profiles are of different devices: /device:TPU:97 before, /device:TPU:112 now
where the time goes in v3:
time: 46.7 us; the launch traced here: 46.6 us
  Pallas kernels  45.8 us (98%)
  between operations  0.8 us (2%)
    pallas_call x1, Pallas kernels, local_step(): pl.pallas_call(functools.partial(attn_kernel, tree, n_grp, scale), out_sh...  44.9 us

profile of v3, /device:TPU:112, one launch (start us, length us, event | category | flops | bytes accessed | tf_op | source)
XLA Modules:
  0.0 46.6 jit_solution(12952659583798077348)
XLA Ops:
  0.6 44.9 %attn.1 = (bf16[1024,128]{1,0:T(8,128)(2,1)S(1)}, bf16[1024,128]{1,0:T(8,128)(2,1)S(1)}, bf16[128,128]{1,0:T(8,128)(2,1)S(1)}, bf16[128,128]{1,0:T(8,128)(2,1)S(1)}) custom-call(bf16[1024,128]{1,0:T(8,128)(2,1)} %bitcast.8, bf16[1024,128]{1,0:T(8,128)(2,1)} %bitcast.9, bf16[128,128]{1,0:T(8,128)(2,1)} %bitcast.10, bf16[128,128]{1,0:T(8,128)(2,1)} %bitcast.11), custom_call_target="tpu_custom_call" | custom-call | tf_op jit(solution)/shard_map/attn/pallas_call | solution.py:422
  45.6 0.8 %store.1 = (bf16[1024,128]{1,0:T(8,128)(2,1)}, bf16[1024,128]{1,0:T(8,128)(2,1)}, bf16[128,128]{1,0:T(8,128)(2,1)}, bf16[128,128]{1,0:T(8,128)(2,1)}) custom-call(bf16[1024,128]{1,0:T(8,128)(2,1)S(1)} %get-tuple-element.12.refs_0_, bf16[1024,128]{1,0:T(8,128)(2,1)S(1)} %get-tuple-element.13.refs_1_, bf16[128,128]{1,0:T(8,128)(2,1)S(1)} %get-tuple-element.14.refs_2_, ...), custom_call_target="tpu_custom_call" | custom-call | tf_op jit(solution)/shard_map/store/pallas_call | solution.py:457

commit v4 on v3

--- a/solution.py
+++ b/solution.py
@@ -16,10 +16,10 @@
 BF16 = jnp.bfloat16
 GRAD, SUM, QUERY = 0, 1, 2
 PLAN = (
-    (GRAD, 15), (GRAD, 11), (GRAD, 7), (GRAD, 12), (SUM, 15), (SUM, 11), (GRAD, 13), (GRAD, 10), (SUM, 12),
-    (GRAD, 9), (SUM, 13), (QUERY, 2), (SUM, 10), (GRAD, 3), (SUM, 7), (SUM, 9), (GRAD, 14), (GRAD, 1), (GRAD, 8),
-    (SUM, 14), (SUM, 1), (QUERY, 2), (GRAD, 5), (GRAD, 2), (SUM, 8), (GRAD, 0), (SUM, 5), (GRAD, 6), (GRAD, 4),
-    (QUERY, 2), (SUM, 6), (QUERY, 2), (QUERY, 2), (SUM, 2), (SUM, 4), (QUERY, 2), (QUERY, 2), (QUERY, 2), (SUM, 3),
+    (GRAD, 15), (GRAD, 11), (GRAD, 12), (SUM, 15), (GRAD, 13), (SUM, 11), (GRAD, 7), (SUM, 12), (GRAD, 14),
+    (SUM, 13), (GRAD, 9), (GRAD, 1), (SUM, 7), (SUM, 14), (GRAD, 10), (SUM, 9), (QUERY, 2), (SUM, 1), (QUERY, 2),
+    (QUERY, 2), (QUERY, 2), (SUM, 10), (GRAD, 5), (GRAD, 4), (GRAD, 8), (GRAD, 6), (QUERY, 2), (SUM, 5), (SUM, 8),
+    (QUERY, 2), (GRAD, 3), (SUM, 6), (GRAD, 2), (QUERY, 2), (GRAD, 0), (SUM, 2), (SUM, 4), (QUERY, 2), (SUM, 3),
 )
 PARENTS = (
     (None, (0, 1), (0, 3), (1, 0), (3, 0), (1, 1), (0, 3), (0, 1), (3, 0), (0, 3), (1, 0), (0, 1), (1, 0), (3, 0), (3, 3), (1, 1)),
@@ -166,7 +166,7 @@
     def tree_copy(tensor, slot):
         hop = tree.parent(tensor, tree.order[slot])
         return remote(part.at[slot, core, tensor], tree_in.at[tensor, slot],
-                      sent_sem.at[2 * tensor, slot], tree_sem.at[tensor, slot], near(hop))
+                      (gather_sem, cross_sem)[tensor].at[slot], tree_sem.at[tensor, slot], near(hop))
 
     def concerns(slot, offsets):
         owner = chip_at(tree.order[slot])
@@ -203,7 +203,7 @@
             return lax.shift_right_logical(jnp.int32(signed), 2 * slot) & 3
         return chip_at((field(xs), field(ys)))
 
-    def score_step(slots, masked):
+    def score_step(slots, masked, with_dp):
         for c, rng in enumerate(chunks):
             m = None if masked else m_buf[:, rng]
             for slot in slots:
@@ -215,7 +215,8 @@
                 s_buf[slot, :, rng] = s
                 top = jnp.max(fold(s), axis=0)
                 m = top if m is None else jnp.maximum(m, top)
-                dp_buf[slot, :, rng] = dot_nn(kv_s[slot, VALUE], do_t[:, rng])
+                if with_dp:
+                    dp_buf[slot, :, rng] = dot_nn(kv_s[slot, VALUE], do_t[:, rng])
             m_buf[:, rng] = m
 
     def value_step(slots):
@@ -250,10 +251,10 @@
         if (last - first) % 2:
             pl.when(active(last - 1))(lambda: body([last - 1]))
 
-    def score_body(slots):
+    def score_body(with_dp, slots):
         for slot in slots:
             cross_copy(slot).wait_recv()
-        score_step(slots, False)
+        score_step(slots, False, with_dp)
 
     def value_body(slots):
         value_step(slots)
@@ -261,7 +262,7 @@
             cross_copy(slot).wait_send()
 
     def score_loop(first, last):
-        pair_loop(first, last, score_body)
+        pair_loop(first, last, functools.partial(score_body, first < n_near))
 
     def value_loop(first, last):
         pair_loop(first, last, value_body)
@@ -277,7 +278,7 @@
         l_buf[...] = jnp.zeros(l_buf.shape, F32)
         acc_buf[...] = jnp.zeros(acc_buf.shape, F32)
         cross_copy(0).wait_recv()
-        score_step([0], True)
+        score_step([0], True, True)
 
     n_next = tree.bounds[2]
     for first, last in ((1, n_next), (n_next, n_near)):
@@ -310,7 +311,8 @@
     def grad_step(slot):
         for rng in chunks:
             p = jnp.exp2(fold(s_buf[slot, :, rng]) * to_log2 - top_buf[:, rng])
-            ds = p * (fold(dp_buf[slot, :, rng]) - d_buf[:, rng])
+            dp = dp_buf[slot, :, rng] if slot < n_near else dot_nn(kv_s[slot, VALUE], do_t[:, rng])
+            ds = p * (fold(dp) - d_buf[:, rng])
             p_buf[:, rng] = p.reshape(width, CHUNK).astype(BF16)
             ds_buf[slot, :, rng] = ds.reshape(width, CHUNK).astype(BF16)
         for h in range(2):
@@ -431,7 +433,7 @@
                 pltpu.VMEM((d_head, rows), BF16),
                 pltpu.VMEM((d_head, rows), BF16),
                 pltpu.VMEM((n_slot, width, rows), F32),
-                pltpu.VMEM((n_slot, width, rows), F32),
+                pltpu.VMEM((tree.n_near, width, rows), F32),
                 pltpu.VMEM((n_slot, width, rows), BF16),
                 pltpu.VMEM((width, rows), BF16),
                 pltpu.VMEM((SUBLANES, rows), F32),
@@ -447,7 +449,7 @@
                 dma_sem((n_slot,)),
                 dma_sem((n_slot,)),
                 dma_sem((2, n_slot)),
-                dma_sem((3, n_slot)),
+                dma_sem((2, n_slot)),
             ],
             compiler_params=pltpu.CompilerParams(
                 vmem_limit_bytes=60 * 1024 * 1024, collective_id=0, has_side_effects=True),

time: 46.7 us -> 45.9 us (0.983)
  the two profiles are of different devices: /device:TPU:112 before, /device:TPU:120 now
where the time goes in v4:
time: 45.9 us; the launch traced here: 45.8 us
  Pallas kernels  45 us (98%)
  between operations  0.8 us (2%)
    pallas_call x1, Pallas kernels, local_step(): pl.pallas_call(functools.partial(attn_kernel, tree, n_grp, scale), out_sh...  44.1 us

profile of v4, /device:TPU:120, one launch (start us, length us, event | category | flops | bytes accessed | tf_op | source)
XLA Modules:
  0.0 45.8 jit_solution(14205507680931740684)
XLA Ops:
  0.6 44.1 %attn.1 = (bf16[1024,128]{1,0:T(8,128)(2,1)S(1)}, bf16[1024,128]{1,0:T(8,128)(2,1)S(1)}, bf16[128,128]{1,0:T(8,128)(2,1)S(1)}, bf16[128,128]{1,0:T(8,128)(2,1)S(1)}) custom-call(bf16[1024,128]{1,0:T(8,128)(2,1)} %bitcast.8, bf16[1024,128]{1,0:T(8,128)(2,1)} %bitcast.9, bf16[128,128]{1,0:T(8,128)(2,1)} %bitcast.10, bf16[128,128]{1,0:T(8,128)(2,1)} %bitcast.11), custom_call_target="tpu_custom_call" | custom-call | tf_op jit(solution)/shard_map/attn/pallas_call | solution.py:424
  44.8 0.8 %store.1 = (bf16[1024,128]{1,0:T(8,128)(2,1)}, bf16[1024,128]{1,0:T(8,128)(2,1)}, bf16[128,128]{1,0:T(8,128)(2,1)}, bf16[128,128]{1,0:T(8,128)(2,1)}) custom-call(bf16[1024,128]{1,0:T(8,128)(2,1)S(1)} %get-tuple-element.12.refs_0_, bf16[1024,128]{1,0:T(8,128)(2,1)S(1)} %get-tuple-element.13.refs_1_, bf16[128,128]{1,0:T(8,128)(2,1)S(1)} %get-tuple-element.14.refs_2_, ...), custom_call_target="tpu_custom_call" | custom-call | tf_op jit(solution)/shard_map/store/pallas_call | solution.py:459

commit v5 on v4

--- a/solution.py
+++ b/solution.py
@@ -19,7 +19,7 @@
     (GRAD, 15), (GRAD, 11), (GRAD, 12), (SUM, 15), (GRAD, 13), (SUM, 11), (GRAD, 7), (SUM, 12), (GRAD, 14),
     (SUM, 13), (GRAD, 9), (GRAD, 1), (SUM, 7), (SUM, 14), (GRAD, 10), (SUM, 9), (QUERY, 2), (SUM, 1), (QUERY, 2),
     (QUERY, 2), (QUERY, 2), (SUM, 10), (GRAD, 5), (GRAD, 4), (GRAD, 8), (GRAD, 6), (QUERY, 2), (SUM, 5), (SUM, 8),
-    (QUERY, 2), (GRAD, 3), (SUM, 6), (GRAD, 2), (QUERY, 2), (GRAD, 0), (SUM, 2), (SUM, 4), (QUERY, 2), (SUM, 3),
+    (QUERY, 2), (GRAD, 3), (SUM, 6), (GRAD, 2), (SUM, 4), (GRAD, 0), (SUM, 2), (SUM, 3), (QUERY, 2), (QUERY, 2),
 )
 PARENTS = (
     (None, (0, 1), (0, 3), (1, 0), (3, 0), (1, 1), (0, 3), (0, 1), (3, 0), (0, 3), (1, 0), (0, 1), (1, 0), (3, 0), (3, 3), (1, 1)),

time: 45.9 us -> 45.7 us (level)
  the two profiles are of different devices: /device:TPU:120 before, /device:TPU:97 now
where the time goes in v5:
time: 45.7 us; the launch traced here: 44.9 us
  Pallas kernels  44.1 us (96%)
  between operations  0.8 us (2%)
    pallas_call x1, Pallas kernels, local_step(): pl.pallas_call(functools.partial(attn_kernel, tree, n_grp, scale), out_sh...  43.3 us

profile of v5, /device:TPU:97, one launch (start us, length us, event | category | flops | bytes accessed | tf_op | source)
XLA Modules:
  0.0 44.9 jit_solution(4444161480701126703)
XLA Ops:
  0.6 43.3 %attn.1 = (bf16[1024,128]{1,0:T(8,128)(2,1)S(1)}, bf16[1024,128]{1,0:T(8,128)(2,1)S(1)}, bf16[128,128]{1,0:T(8,128)(2,1)S(1)}, bf16[128,128]{1,0:T(8,128)(2,1)S(1)}) custom-call(bf16[1024,128]{1,0:T(8,128)(2,1)} %bitcast.8, bf16[1024,128]{1,0:T(8,128)(2,1)} %bitcast.9, bf16[128,128]{1,0:T(8,128)(2,1)} %bitcast.10, bf16[128,128]{1,0:T(8,128)(2,1)} %bitcast.11), custom_call_target="tpu_custom_call" | custom-call | tf_op jit(solution)/shard_map/attn/pallas_call | solution.py:424
  43.9 0.8 %store.1 = (bf16[1024,128]{1,0:T(8,128)(2,1)}, bf16[1024,128]{1,0:T(8,128)(2,1)}, bf16[128,128]{1,0:T(8,128)(2,1)}, bf16[128,128]{1,0:T(8,128)(2,1)}) custom-call(bf16[1024,128]{1,0:T(8,128)(2,1)S(1)} %get-tuple-element.12.refs_0_, bf16[1024,128]{1,0:T(8,128)(2,1)S(1)} %get-tuple-element.13.refs_1_, bf16[128,128]{1,0:T(8,128)(2,1)S(1)} %get-tuple-element.14.refs_2_, ...), custom_call_target="tpu_custom_call" | custom-call | tf_op jit(solution)/shard_map/store/pallas_call | solution.py:459
